TPU v7x, 32 devices: a whole 2x2x4 slice. The times are simulated.
32 devices in a mesh: lat: 8 (over z, core), wave: 4 (over y, x).
Axes of the slice: x: 2, y: 2, z: 4, core: 2. Of those that a mesh axis runs over, the one named last changes fastest.
Arguments:
- spectra: bfloat16 [3, 2, 2, 768, 768], P(None, None, None, 'wave', 'lat'), may hold values from -0.01171875 to 0.01171875
- legendre: bfloat16 [16, 768, 768], P('lat', 'wave'), may hold values from -4 to 4
- wave_m: int32 [768], replicated, may hold values from 0 to 767, each once
- nlon: int32 [16], P('lat'), may hold values from 20 to 3088, as said below
- coriolis: float32 [16], P('lat'), may hold values from -1.5 to 1.5
- gauss_quadrature_weight: float32 [16], P('lat'), may hold values from 0.5 to 5
Outputs:
- tendency: float32 [2, 2, 2, 768, 768], P(None, None, None, 'wave', 'lat')
Inputs may be any that keep to these rules, and one draw needn't show every extreme that they name: `nlon`: each value is 20 + 4 i for a whole number i, and some latitude has 3088. `wave_m`: every wavenumber 0 to 767 stands in exactly one slot.
All inputs are finite; a program needn't handle non-finite values.
Results may differ from a plain program's by a relative error of at most 0.0065.
Values may be sent and summed in bfloat16 or wider, within the bound.
No kernel may reach another device: no remote copies, remote signals or barrier semaphores. Data moves between devices by JAX's collectives and lax.ppermute only.
A program may use at most 64 MiB of HBM per device.

v0:
```python
import jax
import jax.numpy as jnp
from jax import lax
from jax.sharding import PartitionSpec as P

NLON = 3088
lon_block = 512
two_pi = 6.283185307179586


def block_count():
    return (NLON + lon_block - 1) // lon_block


def pick_entry(values, position):
    positions = jnp.arange(values.shape[0], dtype=jnp.int32)
    return jnp.sum(jnp.where(positions == position, values, jnp.zeros_like(values)))


def column_factor(wave_ids, count):
    doubled = jnp.where(wave_ids == 0, jnp.float32(1.0), jnp.float32(2.0))
    return jnp.where(2 * wave_ids < count, doubled, jnp.float32(0.0))


def phase_table(wave_ids, first_place, count):
    places = first_place + jnp.arange(lon_block, dtype=jnp.int32)
    residue = places[:, None] * wave_ids[None, :] % count
    angles = two_pi * residue.astype(jnp.float32) / count.astype(jnp.float32)
    return jnp.concatenate([jnp.cos(angles), jnp.sin(angles)], axis=1).astype(jnp.bfloat16)


def inverse_stack(coefficient, multiplier):
    real_part = coefficient[..., 0, :].astype(jnp.float32) * multiplier
    imag_part = -coefficient[..., 1, :].astype(jnp.float32) * multiplier
    return jnp.concatenate([real_part, imag_part], axis=-1).astype(jnp.bfloat16)


def nonlinear(nodal_samples, rotation, places, count):
    vorticity = nodal_samples[..., 0, :]
    velocity_spread_map = nodal_samples[..., 1, :]
    thermal_state_map = nodal_samples[..., 2, :]
    stretch = -(vorticity + rotation) * velocity_spread_map
    thermal_forcing = -thermal_state_map * velocity_spread_map
    paired = jnp.stack([stretch, thermal_forcing], axis=-2)
    return jnp.where(places < count, paired, jnp.zeros_like(paired)).astype(jnp.bfloat16)


def finish(summed_spectra, multiplier, count, weight):
    halfway = summed_spectra.shape[-1] // 2
    scaling_factor = weight / count.astype(jnp.float32)
    real_part = summed_spectra[..., :halfway] * scaling_factor
    imag_part = -summed_spectra[..., halfway:] * scaling_factor
    paired = jnp.stack([real_part, imag_part], axis=-2)
    return jnp.where(multiplier > 0, paired, jnp.zeros_like(paired)).astype(jnp.bfloat16)


def grid_row(piled_arrays, wave_ids, count, rotation, weight, multiplier):

    def one_block(running, block_index):
        first_place = block_index * lon_block
        phases = phase_table(wave_ids, first_place, count)
        nodal_samples = lax.dot_general(
            piled_arrays, phases, (((1,), (1,)), ((), ())), preferred_element_type=jnp.float32
        )
        nodal_samples = nodal_samples.reshape(-1, 3, lon_block)
        places = first_place + jnp.arange(lon_block, dtype=jnp.int32)
        products = nonlinear(nodal_samples, rotation, places, count).reshape(-1, lon_block)
        return (running + jnp.dot(products, phases, preferred_element_type=jnp.float32), None)

    zero_sums = jnp.zeros((piled_arrays.shape[0] // 3 * 2, piled_arrays.shape[1]), jnp.float32)
    summed_spectra, unused = lax.scan(
        one_block, zero_sums, jnp.arange(block_count(), dtype=jnp.int32)
    )
    return finish(summed_spectra.reshape(-1, 2, piled_arrays.shape[1]), multiplier, count, weight)


def local(spectra, legendre, wave_m, nlon, coriolis, gauss_quadrature_weight):
    band_lats, slot_count, wave_total = legendre.shape
    lev_count = spectra.shape[1]
    band_rows = band_lats * lev_count
    wave_rank = lax.axis_index("wave")
    local_ids = lax.dynamic_slice_in_dim(wave_m, wave_rank * slot_count, slot_count, 0)
    totals = jnp.arange(wave_total, dtype=jnp.int32)
    masked = jnp.where(
        totals[None, None, :] >= local_ids[None, :, None], legendre, jnp.zeros_like(legendre)
    )

    def row_facts(row_number):
        latitude_row = row_number // lev_count
        return (
            pick_entry(nlon, latitude_row),
            pick_entry(coriolis, latitude_row),
            pick_entry(gauss_quadrature_weight, latitude_row),
        )

    band_part = masked
    fourier = jnp.einsum(
        "lsn,fvpsn->lvfps",
        band_part,
        lax.all_gather(spectra, "lat", axis=4, tiled=True),
        preferred_element_type=jnp.float32,
    ).astype(jnp.bfloat16)
    fourier = fourier.reshape(band_rows, 3, 2, slot_count)
    gathered = lax.all_to_all(fourier, "wave", split_axis=0, concat_axis=3, tiled=True)
    owned_latitude_rows = gathered.shape[0]

    def full_row(inputs):
        coefficient, offset = inputs
        count, rotation, weight = row_facts(wave_rank * owned_latitude_rows + offset)
        multiplier = column_factor(wave_m, count)
        piled_arrays = inverse_stack(coefficient, multiplier)
        return grid_row(piled_arrays, wave_m, count, rotation, weight, multiplier)[0]

    local_rows = lax.map(full_row, (gathered, jnp.arange(owned_latitude_rows, dtype=jnp.int32)))
    returned = lax.all_to_all(local_rows, "wave", split_axis=3, concat_axis=0, tiled=True)
    returned = returned.reshape(band_lats, lev_count, 2, 2, slot_count)
    turned = lax.all_to_all(masked, "lat", split_axis=2, concat_axis=0, tiled=True)
    band_part = turned
    return jnp.einsum(
        "lsn,lvqps->qvpsn",
        band_part,
        lax.all_gather(returned, "lat", axis=0, tiled=True),
        preferred_element_type=jnp.float32,
    )


def solution(mesh):
    placed = (
        P(None, None, None, "wave", "lat"),
        P("lat", "wave", None),
        P(),
        P("lat"),
        P("lat"),
        P("lat"),
    )
    return jax.shard_map(
        local,
        mesh=mesh,
        in_specs=placed,
        out_specs=P(None, None, None, "wave", "lat"),
        check_vma=False,
    )
```

profile of v0, /device:TPU:0, one launch (start us, length us, event | category | flops | bytes accessed | tf_op | source)
XLA Modules:
  0.0 325.8 jit_solution(5381453114664748880)
XLA Ops:
  6.5 2.2 copy.49
  8.7 0.6 copy.48
  9.6 1.3 fusion.32
  11.0 1.5 copy.61
  12.5 0.6 select_reduce_fusion.2
  13.8 2.2 broadcast_select_fusion
  16.0 47.0 %all-gather.2.cloned.1.call-done = bf16[3,2,2,192,768]{3,2,1,0,4:T(2,128)(2,1)} async-done(((bf16[3,2,2,192,96]{3,2,1,0,4:T(2,128)(2,1)}), bf16[3,2,2,192,768]{3,2,1,0,4:T(2,128)(2,1)}) %all-gather.2.cloned.1.call-update) | async-done | bytes 3538960 | tf_op jit(solution)/shard_map/all_gather | solution.py:100
  62.9 16.6 %copy.51 = bf16[3,2,2,192,768]{4,0,2,1,3:T(4,128)(2,1)} copy(bf16[3,2,2,192,768]{3,2,1,0,4:T(2,128)(2,1)} %all-gather.2.cloned.1.call-done) | data formatting | bytes 7077888 | tf_op jit(solution)/shard_map/all_gather | solution.py:100
  79.6 23.1 %fusion.19 = bf16[2,2,3,2,192]{2,0,3,1,4:T(2,128)(2,1)S(1)} fusion(bf16[2,192,768,1,1]{2,0,4,3,1:T(2,128)(2,1)S(1)} %copy.61, bf16[3,2,2,192,768]{4,0,2,1,3:T(4,128)(2,1)} %copy.51), kind=kOutput, calls=%fused_computation.33 | convolution fusion | flops 7082496 | bytes 4137984 | tf_op jit(solution)/shard_map/lsn,fvpsn->lvfps/dot_general | solution.py:97
  102.7 1.1 copy.52
  103.8 3.6 %all-to-all-start = ((bf16[4,3,2,192]{3,2,1,0:T(2,128)(2,1)}), bf16[4,3,2,192]{3,2,1,0:T(2,128)(2,1)S(1)}, u32[]{:S(2)}, u32[]{:S(2)}) async-start(bf16[4,3,2,192]{3,2,1,0:T(2,128)(2,1)} %bitcast.2), calls=%async_computation | async-start | bytes 24576 | tf_op jit(solution)/shard_map/all_to_all | solution.py:104
  107.4 0.7 select_reduce_fusion
  110.7 1.5 all-to-all-done
  112.1 3.5 %all-to-all-start.2 = ((bf16[2,192,768]{1,0,2:T(2,128)(2,1)}), bf16[2,192,768]{1,0,2:T(2,128)(2,1)S(1)}, u32[]{:S(2)}, u32[]{:S(2)}) async-start(bf16[2,192,768]{1,0,2:T(2,128)(2,1)} %broadcast_select_fusion), calls=%async_computation.2 | async-start | bytes 1572864 | tf_op jit(solution)/shard_map/all_to_all | solution.py:117
  115.8 175.8 %while.20 = (s32[]{:T(128)}, f32[2,1536]{1,0:T(2,128)S(1)}, s32[7]{0:T(128)S(1)}, s32[]{:T(128)}, s32[768]{0:T(1024)S(1)}, /*index=5*/s32[]{:T(128)}, pred[]{:T(...) while((s32[]{:T(128)}, f32[2,1536]{1,0:T(2,128)S(1)}, ...), condition=%wide.region_3.4_spmd.clone, body=%wide.region_2.3_spmd.clone.sunk | while | flops 19283972 | bytes 4777152 | solution.py:71
  117.8 21.8 %cosine_convert_fusion.2 = (bf16[512,768]{1,0:T(8,128)(2,1)S(1)}, bf16[512,768]{1,0:T(8,128)(2,1)S(1)}) fusion(f32[]{:T(128)} %get-tuple-element.295, pred[]{:T(512)} %get-tuple-element.294, s32[]{:T(128)} %get-tuple-element.293, s32[768]{0:T(1024)S(1)} %get-tuple-element.292, s32[512]{0:T(512)S(1)} %iota_add_fusion.2), kind=kLoop, calls=%fused_computation.7.clone.1 | loop fusion | flops 5111808 | bytes 1577993 | tf_op jit(solution)/shard_map/convert
  142.2 0.6 broadcast_compare_fusion.3
  142.9 21.8 %cosine_convert_fusion.2 = (bf16[512,768]{1,0:T(8,128)(2,1)S(1)}, bf16[512,768]{1,0:T(8,128)(2,1)S(1)}) fusion(f32[]{:T(128)} %get-tuple-element.295, pred[]{:T(512)} %get-tuple-element.294, s32[]{:T(128)} %get-tuple-element.293, s32[768]{0:T(1024)S(1)} %get-tuple-element.292, s32[512]{0:T(512)S(1)} %iota_add_fusion.2), kind=kLoop, calls=%fused_computation.7.clone.1 | loop fusion | flops 5111808 | bytes 1577993 | tf_op jit(solution)/shard_map/convert
  168.0 21.8 %cosine_convert_fusion.2 = (bf16[512,768]{1,0:T(8,128)(2,1)S(1)}, bf16[512,768]{1,0:T(8,128)(2,1)S(1)}) fusion(f32[]{:T(128)} %get-tuple-element.295, pred[]{:T(512)} %get-tuple-element.294, s32[]{:T(128)} %get-tuple-element.293, s32[768]{0:T(1024)S(1)} %get-tuple-element.292, s32[512]{0:T(512)S(1)} %iota_add_fusion.2), kind=kLoop, calls=%fused_computation.7.clone.1 | loop fusion | flops 5111808 | bytes 1577993 | tf_op jit(solution)/shard_map/convert
  192.5 0.6 broadcast_compare_fusion.3
  193.1 21.8 %cosine_convert_fusion.2 = (bf16[512,768]{1,0:T(8,128)(2,1)S(1)}, bf16[512,768]{1,0:T(8,128)(2,1)S(1)}) fusion(f32[]{:T(128)} %get-tuple-element.295, pred[]{:T(512)} %get-tuple-element.294, s32[]{:T(128)} %get-tuple-element.293, s32[768]{0:T(1024)S(1)} %get-tuple-element.292, s32[512]{0:T(512)S(1)} %iota_add_fusion.2), kind=kLoop, calls=%fused_computation.7.clone.1 | loop fusion | flops 5111808 | bytes 1577993 | tf_op jit(solution)/shard_map/convert
  218.2 21.8 %cosine_convert_fusion.2 = (bf16[512,768]{1,0:T(8,128)(2,1)S(1)}, bf16[512,768]{1,0:T(8,128)(2,1)S(1)}) fusion(f32[]{:T(128)} %get-tuple-element.295, pred[]{:T(512)} %get-tuple-element.294, s32[]{:T(128)} %get-tuple-element.293, s32[768]{0:T(1024)S(1)} %get-tuple-element.292, s32[512]{0:T(512)S(1)} %iota_add_fusion.2), kind=kLoop, calls=%fused_computation.7.clone.1 | loop fusion | flops 5111808 | bytes 1577993 | tf_op jit(solution)/shard_map/convert
  243.3 21.8 %cosine_convert_fusion.2 = (bf16[512,768]{1,0:T(8,128)(2,1)S(1)}, bf16[512,768]{1,0:T(8,128)(2,1)S(1)}) fusion(f32[]{:T(128)} %get-tuple-element.295, pred[]{:T(512)} %get-tuple-element.294, s32[]{:T(128)} %get-tuple-element.293, s32[768]{0:T(1024)S(1)} %get-tuple-element.292, s32[512]{0:T(512)S(1)} %iota_add_fusion.2), kind=kLoop, calls=%fused_computation.7.clone.1 | loop fusion | flops 5111808 | bytes 1577993 | tf_op jit(solution)/shard_map/convert
  268.5 21.8 %cosine_convert_fusion.2 = (bf16[512,768]{1,0:T(8,128)(2,1)S(1)}, bf16[512,768]{1,0:T(8,128)(2,1)S(1)}) fusion(f32[]{:T(128)} %get-tuple-element.295, pred[]{:T(512)} %get-tuple-element.294, s32[]{:T(128)} %get-tuple-element.293, s32[768]{0:T(1024)S(1)} %get-tuple-element.292, s32[512]{0:T(512)S(1)} %iota_add_fusion.2), kind=kLoop, calls=%fused_computation.7.clone.1 | loop fusion | flops 5111808 | bytes 1577993 | tf_op jit(solution)/shard_map/convert
  292.2 1.1 reshape.136
  293.3 3.2 all-to-all-start.1
  296.5 1.0 copy.58
  297.5 3.7 %all-to-all-done.1 = bf16[4,2,384]{2,1,0:T(2,128)(2,1)S(1)} async-done(((bf16[4,2,384]{2,1,0:T(2,128)(2,1)}), bf16[4,2,384]{2,1,0:T(2,128)(2,1)S(1)}, u32[]{:S(2)}, u32[]{:S(2)}) %all-to-all-start.1) | async-done | bytes 6176 | tf_op jit(solution)/shard_map/all_to_all | solution.py:115
  301.1 0.8 reshape.137
  302.3 14.4 %all_gather.7 = bf16[16,2,2,2,192]{4,3,2,1,0:T(2,128)(2,1)S(1)} all-gather(bf16[2,2,2,2,192]{4,3,2,1,0:T(2,128)(2,1)S(1)} %bitcast.68), channel_id=1, replica_groups=mesh['lat'=8,'wave'=4] {'lat'}, dimensions={0}, use_global_device_ids=true | all-gather | bytes 55296 | tf_op jit(solution)/shard_map/all_gather | solution.py:122
  317.2 0.7 convolution_bitcast_fusion.1
  317.9 1.0 copy.60
  (69 shorter events, 19.6 us)
Async XLA Ops:
  6.5 2.2 copy-start
  6.5 2.9 copy-start.1
  6.5 56.4 %all-gather.2.cloned.1.call-start = ((), (), s32[]{:S(2)}) async-start(), calls=%async_computation.3 | async-start | bytes 5308416 | tf_op jit(solution)/shard_map/all_gather | solution.py:100
  9.6 2.9 copy-start.4
  79.6 27.8 %copy-start.2 = (f32[2]{0:T(128)S(1)}, f32[2]{0:T(128)}, u32[]{:S(2)}) copy-start(f32[2]{0:T(128)} %param.13) | copy-start | bytes 28
  79.6 27.8 %copy-start.3 = (f32[2]{0:T(128)S(1)}, f32[2]{0:T(128)}, u32[]{:S(2)}) copy-start(f32[2]{0:T(128)} %param.12) | copy-start | bytes 28
  103.8 8.3 %all-to-all-start = ((bf16[4,3,2,192]{3,2,1,0:T(2,128)(2,1)}), bf16[4,3,2,192]{3,2,1,0:T(2,128)(2,1)S(1)}, u32[]{:S(2)}, u32[]{:S(2)}) async-start(bf16[4,3,2,192]{3,2,1,0:T(2,128)(2,1)} %bitcast.2), calls=%async_computation | async-start | bytes 24576 | tf_op jit(solution)/shard_map/all_to_all | solution.py:104
  112.1 181.1 %all-to-all-start.2 = ((bf16[2,192,768]{1,0,2:T(2,128)(2,1)}), bf16[2,192,768]{1,0,2:T(2,128)(2,1)S(1)}, u32[]{:S(2)}, u32[]{:S(2)}) async-start(bf16[2,192,768]{1,0,2:T(2,128)(2,1)} %broadcast_select_fusion), calls=%async_computation.2 | async-start | bytes 1572864 | tf_op jit(solution)/shard_map/all_to_all | solution.py:117
  293.3 7.9 %all-to-all-start.1 = ((bf16[4,2,384]{2,1,0:T(2,128)(2,1)}), bf16[4,2,384]{2,1,0:T(2,128)(2,1)S(1)}, u32[]{:S(2)}, u32[]{:S(2)}) async-start(bf16[4,2,384]{2,1,0:T(2,128)(2,1)} %reshape.136), calls=%async_computation.1 | async-start | bytes 12288 | tf_op jit(solution)/shard_map/all_to_all | solution.py:115
Sparse Core Ops, SparseCore 0:
  9.0 53.9 all-gather.1
where the time goes:
time: 327 us; the launch traced here: 326 us
  other arithmetic  167 us (51%)
  waiting for transfers between devices  52.1 us (16%)
  local copies, waits for them, and re-layouts  31.6 us (10%)
  matrix products  29.6 us (9%)
  between operations  16.2 us (5%)
  blocking collectives  14.4 us (4%)
  starting transfers between devices  10.4 us (3%)
  loops' own time  4.72 us (1%)
    another operation x8, other arithmetic  153 us
    all_gather x1, waiting for transfers between devices, local(): lax.all_gather(spectra, 'lat', axis=4, tiled=True)  47 us
    dot_general x1, matrix products, local(): jnp.einsum('lsn,fvpsn->lvfps', band_part, lax.all_gather(spectra, 'lat',...  23.1 us
    all_gather x1, local copies, waits for them, and re-layouts, local(): lax.all_gather(spectra, 'lat', axis=4, tiled=True)  16.6 us
    all_gather x1, blocking collectives, local(): lax.all_gather(returned, 'lat', axis=0, tiled=True)  14.4 us
  transfers between devices with their start and end apart: 4, of which 3 were waited for; matrix products, arithmetic and copies ran while one was open for 56% of the time, Pallas kernels for 0%

commit v1 on v0

--- a/solution.py
+++ b/solution.py
@@ -6,6 +6,16 @@
 NLON = 3088
 lon_block = 512
 two_pi = 6.283185307179586
+
+
+def collect(x, axis, dim):
+    ways, here, step = (lax.axis_size(axis), lax.axis_index(axis), x.shape[dim])
+    lengths = [n * ways if d == dim else n for d, n in enumerate(x.shape)]
+    full = lax.dynamic_update_slice_in_dim(jnp.zeros(lengths, x.dtype), x, here * step, axis=dim)
+    for far in range(1, ways):
+        x = lax.ppermute(x, axis, [(d, (d + 1) % ways) for d in range(ways)])
+        full = lax.dynamic_update_slice_in_dim(full, x, (here - far) % ways * step, axis=dim)
+    return full
 
 
 def block_count():
@@ -97,7 +107,7 @@
     fourier = jnp.einsum(
         "lsn,fvpsn->lvfps",
         band_part,
-        lax.all_gather(spectra, "lat", axis=4, tiled=True),
+        collect(spectra, "lat", 4),
         preferred_element_type=jnp.float32,
     ).astype(jnp.bfloat16)
     fourier = fourier.reshape(band_rows, 3, 2, slot_count)

time: 327 us -> 1220 us (3.73)
  local copies, waits for them, and re-layouts: 31.6 us -> 833 us
  starting transfers between devices: 10.4 us -> 108 us
  between operations: 16.2 us -> 2.74 us
    dynamic_update_slice x0 -> x8, local copies, waits for them, and re-layouts: none -> 806 us  [the longest x7 783 us: collect(): lax.dynamic_update_slice_in_dim(full, x, (here - far) % ways * step, axis...]
    ppermute x0 -> x7, starting transfers between devices: none -> 97.2 us  [collect(): x = lax.ppermute(x, axis, [(d, (d + 1) % ways) for d in range(ways)])]
    ppermute x0 -> x7, waiting for transfers between devices: none -> 55.6 us  [collect(): x = lax.ppermute(x, axis, [(d, (d + 1) % ways) for d in range(ways)])]
    all_gather x1 -> x0, waiting for transfers between devices: 47 us -> none  [local(): lax.all_gather(spectra, 'lat', axis=4, tiled=True)]
    all_gather x1 -> x0, local copies, waits for them, and re-layouts: 16.6 us -> none  [local(): lax.all_gather(spectra, 'lat', axis=4, tiled=True)]
  transfers between devices with their start and end apart: 4 -> 10, of which waited for: 3 -> 7; matrix products, arithmetic and copies ran while one was open for 56% -> 72% of each run, Pallas kernels for 0% -> 0%
where the time goes in v1:
time: 1220 us
  local copies, waits for them, and re-layouts  833 us (68%)
  other arithmetic  167 us (14%)
  starting transfers between devices  108 us (9%)
  waiting for transfers between devices  60.9 us (5%)
  matrix products  29.6 us (2%)
  blocking collectives  14.5 us (1%)
    dynamic_update_slice x7, local copies, waits for them, and re-layouts, collect(): lax.dynamic_update_slice_in_dim(full, x, (here - far) % ways * step, axis...  783 us
    another operation x8, other arithmetic  153 us
    ppermute x7, starting transfers between devices, collect(): x = lax.ppermute(x, axis, [(d, (d + 1) % ways) for d in range(ways)])  97.2 us
    ppermute x7, waiting for transfers between devices, collect(): x = lax.ppermute(x, axis, [(d, (d + 1) % ways) for d in range(ways)])  55.6 us
  transfers between devices with their start and end apart: 10, of which 7 were waited for; matrix products, arithmetic and copies ran while one was open for 72% of the time, Pallas kernels for 0%

profile of v1, /device:TPU:0, one launch (start us, length us, event | category | flops | bytes accessed | tf_op | source)
XLA Modules:
  0.0 1220.1 jit_solution(8548029750530250746)
XLA Ops:
  0.5 11.8 collective-permute-done
  12.3 11.1 collective-permute-done.1
  23.4 11.1 collective-permute-done.2
  34.5 11.1 collective-permute-done.3
  46.4 10.4 collective-permute-done.4
  60.7 2.3 copy.93
  63.1 3.4 broadcast_in_dim.52
  66.4 23.2 %dynamic_update_slice.27 = bf16[3,2,2,192,768]{4,0,2,1,3:T(4,128)(2,1)} dynamic-update-slice(bf16[3,2,2,192,768]{4,0,2,1,3:T(4,128)(2,1)} %broadcast_in_dim.52, bf16[3,2,2,192,96]{4,0,2,1,3:T(4,128)(2,1)S(1)} %copy.74, s32[]{:T(128)} %constant.134.clone.1, s32[]{:T(128)} %constant.134.clone.1, s32[]{:T(128)} %constant.134.clone.1, s32[]{:T(128)} %constant.134.clone.1, s32[]{:T(128)S(6)} %select_n.130) | dynamic-update-slice | bytes 884740 | tf_op jit(solution)/shard_map/dynamic_update_slice | solution.py:14
  90.3 96.7 %collective-permute-start.6 = (bf16[3,2,2,192,96]{4,3,2,1,0:T(8,128)(2,1)}, bf16[3,2,2,192,96]{4,3,2,1,0:T(8,128)(2,1)}, u32[]{:S(2)}, u32[]{:S(2)}) collective-permute-start(bf16[3,2,2,192,96]{4,3,2,1,0:T(8,128)(2,1)} %collective-permute-done.5), channel_id=1, source_target_pairs={{0,4},{4,8},{8,12},{12,16},{16,20},{20,24},{24,28},{28,0},{1,5},{5... | collective-permute-start | bytes 1327112 | tf_op jit(solution)/shard_map/ppermute | solution.py:16
  187.5 2.2 broadcast_select_fusion
  190.2 126.3 %dynamic_update_slice.28 = bf16[3,2,2,192,768]{4,0,2,1,3:T(4,128)(2,1)} dynamic-update-slice(bf16[3,2,2,192,768]{4,0,2,1,3:T(4,128)(2,1)} %dynamic_update_slice.27, bf16[3,2,2,192,96]{4,0,2,1,3:T(4,128)(2,1)S(1)} %copy.75, s32[]{:T(128)} %constant.134.clone.1, s32[]{:T(128)} %constant.134.clone.1, s32[]{:T(128)} %constant.134.clone.1, s32[]{:T(128)} %constant.134.clone.1, s32[]{:T(128)S(6)} %select_n.132) | dynamic-update-slice | bytes 884740 | tf_op jit(solution)/shard_map/dynamic_update_slice | solution.py:17
  317.0 126.7 %dynamic_update_slice.29 = bf16[3,2,2,192,768]{4,0,2,1,3:T(4,128)(2,1)} dynamic-update-slice(bf16[3,2,2,192,768]{4,0,2,1,3:T(4,128)(2,1)} %dynamic_update_slice.28, bf16[3,2,2,192,96]{4,0,2,1,3:T(4,128)(2,1)S(1)} %copy.76, s32[]{:T(128)} %constant.134.clone.1, s32[]{:T(128)} %constant.134.clone.1, s32[]{:T(128)} %constant.134.clone.1, s32[]{:T(128)} %constant.134.clone.1, s32[]{:T(128)S(6)} %select_n.134) | dynamic-update-slice | bytes 884740 | tf_op jit(solution)/shard_map/dynamic_update_slice | solution.py:17
  444.2 126.7 %dynamic_update_slice.30 = bf16[3,2,2,192,768]{4,0,2,1,3:T(4,128)(2,1)} dynamic-update-slice(bf16[3,2,2,192,768]{4,0,2,1,3:T(4,128)(2,1)} %dynamic_update_slice.29, bf16[3,2,2,192,96]{4,0,2,1,3:T(4,128)(2,1)S(1)} %copy.77, s32[]{:T(128)} %constant.134.clone.1, s32[]{:T(128)} %constant.134.clone.1, s32[]{:T(128)} %constant.134.clone.1, s32[]{:T(128)} %constant.134.clone.1, s32[]{:T(128)S(6)} %select_n.136) | dynamic-update-slice | bytes 884740 | tf_op jit(solution)/shard_map/dynamic_update_slice | solution.py:17
  571.4 23.2 %dynamic_update_slice.31 = bf16[3,2,2,192,768]{4,0,2,1,3:T(4,128)(2,1)} dynamic-update-slice(bf16[3,2,2,192,768]{4,0,2,1,3:T(4,128)(2,1)} %dynamic_update_slice.30, bf16[3,2,2,192,96]{4,0,2,1,3:T(4,128)(2,1)S(1)} %copy.78, s32[]{:T(128)} %constant.134.clone.1, s32[]{:T(128)} %constant.134.clone.1, s32[]{:T(128)} %constant.134.clone.1, s32[]{:T(128)} %constant.134.clone.1, s32[]{:T(128)S(6)} %select_n.138) | dynamic-update-slice | bytes 884740 | tf_op jit(solution)/shard_map/dynamic_update_slice | solution.py:17
  596.2 126.7 %dynamic_update_slice.32 = bf16[3,2,2,192,768]{4,0,2,1,3:T(4,128)(2,1)} dynamic-update-slice(bf16[3,2,2,192,768]{4,0,2,1,3:T(4,128)(2,1)} %dynamic_update_slice.31, bf16[3,2,2,192,96]{4,0,2,1,3:T(4,128)(2,1)S(1)} %copy.79, s32[]{:T(128)} %constant.134.clone.1, s32[]{:T(128)} %constant.134.clone.1, s32[]{:T(128)} %constant.134.clone.1, s32[]{:T(128)} %constant.134.clone.1, s32[]{:T(128)S(6)} %select_n.140) | dynamic-update-slice | bytes 884740 | tf_op jit(solution)/shard_map/dynamic_update_slice | solution.py:17
  724.5 126.7 %dynamic_update_slice.33 = bf16[3,2,2,192,768]{4,0,2,1,3:T(4,128)(2,1)} dynamic-update-slice(bf16[3,2,2,192,768]{4,0,2,1,3:T(4,128)(2,1)} %dynamic_update_slice.32, bf16[3,2,2,192,96]{4,0,2,1,3:T(4,128)(2,1)S(1)} %copy.80, s32[]{:T(128)} %constant.134.clone.1, s32[]{:T(128)} %constant.134.clone.1, s32[]{:T(128)} %constant.134.clone.1, s32[]{:T(128)} %constant.134.clone.1, s32[]{:T(128)S(6)} %select_n.142) | dynamic-update-slice | bytes 884740 | tf_op jit(solution)/shard_map/dynamic_update_slice | solution.py:17
  852.8 126.7 %dynamic_update_slice.34 = bf16[3,2,2,192,768]{4,0,2,1,3:T(4,128)(2,1)} dynamic-update-slice(bf16[3,2,2,192,768]{4,0,2,1,3:T(4,128)(2,1)} %dynamic_update_slice.33, bf16[3,2,2,192,96]{4,0,2,1,3:T(4,128)(2,1)S(1)} %copy.81, s32[]{:T(128)} %constant.134.clone.1, s32[]{:T(128)} %constant.134.clone.1, s32[]{:T(128)} %constant.134.clone.1, s32[]{:T(128)} %constant.134.clone.1, s32[]{:T(128)S(6)} %select_n.144) | dynamic-update-slice | bytes 884740 | tf_op jit(solution)/shard_map/dynamic_update_slice | solution.py:17
  979.5 23.1 %fusion.19 = bf16[2,2,3,2,192]{2,0,3,1,4:T(2,128)(2,1)S(1)} fusion(bf16[3,2,2,192,768]{4,0,2,1,3:T(4,128)(2,1)} %dynamic_update_slice.34, bf16[2,192,768,1,1]{2,0,4,3,1:T(2,128)(2,1)S(1)} %copy-done.7), kind=kOutput, calls=%fused_computation.33 | convolution fusion | flops 7082496 | bytes 4137984 | tf_op jit(solution)/shard_map/lsn,fvpsn->lvfps/dot_general | solution.py:107
  1003.7 3.7 all-to-all-start
  1010.5 1.7 all-to-all-done
  1012.2 3.8 all-to-all-start.2
  1016.2 176.5 %while.20 = (s32[]{:T(128)}, f32[2,1536]{1,0:T(2,128)S(1)}, s32[7]{0:T(128)S(1)}, s32[]{:T(128)}, s32[768]{0:T(1024)S(1)}, /*index=5*/s32[]{:T(128)}, pred[]{:T(...) while((s32[]{:T(128)}, f32[2,1536]{1,0:T(2,128)S(1)}, ...), condition=%wide.region_3.4_spmd.clone, body=%wide.region_2.3_spmd.clone.sunk | while | flops 19283972 | bytes 4777144 | solution.py:81
  1017.5 21.8 %cosine_convert_fusion.2 = (bf16[512,768]{1,0:T(8,128)(2,1)S(1)}, bf16[512,768]{1,0:T(8,128)(2,1)S(1)}) fusion(f32[]{:T(128)} %get-tuple-element.295, pred[]{:T(512)} %get-tuple-element.294, s32[]{:T(128)} %get-tuple-element.293, s32[768]{0:T(1024)S(1)} %get-tuple-element.292, s32[512]{0:T(512)S(1)} %iota_add_fusion.2), kind=kLoop, calls=%fused_computation.7.clone.1 | loop fusion | flops 5111808 | bytes 1577993 | tf_op jit(solution)/shard_map/convert
  1042.7 21.8 %cosine_convert_fusion.2 = (bf16[512,768]{1,0:T(8,128)(2,1)S(1)}, bf16[512,768]{1,0:T(8,128)(2,1)S(1)}) fusion(f32[]{:T(128)} %get-tuple-element.295, pred[]{:T(512)} %get-tuple-element.294, s32[]{:T(128)} %get-tuple-element.293, s32[768]{0:T(1024)S(1)} %get-tuple-element.292, s32[512]{0:T(512)S(1)} %iota_add_fusion.2), kind=kLoop, calls=%fused_computation.7.clone.1 | loop fusion | flops 5111808 | bytes 1577993 | tf_op jit(solution)/shard_map/convert
  1067.9 21.8 %cosine_convert_fusion.2 = (bf16[512,768]{1,0:T(8,128)(2,1)S(1)}, bf16[512,768]{1,0:T(8,128)(2,1)S(1)}) fusion(f32[]{:T(128)} %get-tuple-element.295, pred[]{:T(512)} %get-tuple-element.294, s32[]{:T(128)} %get-tuple-element.293, s32[768]{0:T(1024)S(1)} %get-tuple-element.292, s32[512]{0:T(512)S(1)} %iota_add_fusion.2), kind=kLoop, calls=%fused_computation.7.clone.1 | loop fusion | flops 5111808 | bytes 1577993 | tf_op jit(solution)/shard_map/convert
  1093.1 21.8 %cosine_convert_fusion.2 = (bf16[512,768]{1,0:T(8,128)(2,1)S(1)}, bf16[512,768]{1,0:T(8,128)(2,1)S(1)}) fusion(f32[]{:T(128)} %get-tuple-element.295, pred[]{:T(512)} %get-tuple-element.294, s32[]{:T(128)} %get-tuple-element.293, s32[768]{0:T(1024)S(1)} %get-tuple-element.292, s32[512]{0:T(512)S(1)} %iota_add_fusion.2), kind=kLoop, calls=%fused_computation.7.clone.1 | loop fusion | flops 5111808 | bytes 1577993 | tf_op jit(solution)/shard_map/convert
  1118.4 21.8 %cosine_convert_fusion.2 = (bf16[512,768]{1,0:T(8,128)(2,1)S(1)}, bf16[512,768]{1,0:T(8,128)(2,1)S(1)}) fusion(f32[]{:T(128)} %get-tuple-element.295, pred[]{:T(512)} %get-tuple-element.294, s32[]{:T(128)} %get-tuple-element.293, s32[768]{0:T(1024)S(1)} %get-tuple-element.292, s32[512]{0:T(512)S(1)} %iota_add_fusion.2), kind=kLoop, calls=%fused_computation.7.clone.1 | loop fusion | flops 5111808 | bytes 1577993 | tf_op jit(solution)/shard_map/convert
  1143.6 21.8 %cosine_convert_fusion.2 = (bf16[512,768]{1,0:T(8,128)(2,1)S(1)}, bf16[512,768]{1,0:T(8,128)(2,1)S(1)}) fusion(f32[]{:T(128)} %get-tuple-element.295, pred[]{:T(512)} %get-tuple-element.294, s32[]{:T(128)} %get-tuple-element.293, s32[768]{0:T(1024)S(1)} %get-tuple-element.292, s32[512]{0:T(512)S(1)} %iota_add_fusion.2), kind=kLoop, calls=%fused_computation.7.clone.1 | loop fusion | flops 5111808 | bytes 1577993 | tf_op jit(solution)/shard_map/convert
  1168.8 21.8 %cosine_convert_fusion.2 = (bf16[512,768]{1,0:T(8,128)(2,1)S(1)}, bf16[512,768]{1,0:T(8,128)(2,1)S(1)}) fusion(f32[]{:T(128)} %get-tuple-element.295, pred[]{:T(512)} %get-tuple-element.294, s32[]{:T(128)} %get-tuple-element.293, s32[768]{0:T(1024)S(1)} %get-tuple-element.292, s32[512]{0:T(512)S(1)} %iota_add_fusion.2), kind=kLoop, calls=%fused_computation.7.clone.1 | loop fusion | flops 5111808 | bytes 1577993 | tf_op jit(solution)/shard_map/convert
  1194.3 3.2 all-to-all-start.1
  1198.5 3.7 all-to-all-done.1
  1203.4 14.5 %all_gather.3 = bf16[16,2,2,2,192]{4,3,2,1,0:T(2,128)(2,1)S(1)} all-gather(bf16[2,2,2,2,192]{4,3,2,1,0:T(2,128)(2,1)S(1)} %bitcast.68), channel_id=1, replica_groups=mesh['lat'=8,'wave'=4] {'lat'}, dimensions={0}, use_global_device_ids=true | all-gather | bytes 55296 | tf_op jit(solution)/shard_map/all_gather | solution.py:132
  (109 shorter events, 40.1 us)
Async XLA Ops:
  0.0 58.7 %copy-start = (bf16[2,192,768]{2,1,0:T(8,128)(2,1)S(1)}, bf16[2,192,768]{2,1,0:T(8,128)(2,1)}, u32[]{:S(2)}) copy-start(bf16[2,192,768]{2,1,0:T(8,128)(2,1)} %param.9) | copy-start | bytes 1769476
  0.0 12.3 %collective-permute-start = (bf16[3,2,2,192,96]{4,3,2,1,0:T(8,128)(2,1)}, bf16[3,2,2,192,96]{4,3,2,1,0:T(8,128)(2,1)S(1)}, u32[]{:S(2)}, u32[]{:S(2)}) collective-permute-start(bf16[3,2,2,192,96]{4,3,2,1,0:T(8,128)(2,1)} %param.8), channel_id=1, source_target_pairs={{0,4},{4,8},{8,12},{12,16},{16,20},{20,24},{24,28},{28,0},{1,5},{5... | collective-permute-start | bytes 1327112 | tf_op jit(solution)/shard_map/ppermute | solution.py:16
  12.3 11.1 collective-permute-start.1
  23.4 33.6 %copy-start.1 = (bf16[3,2,2,192,96]{4,3,2,1,0:T(8,128)(2,1)}, bf16[3,2,2,192,96]{4,3,2,1,0:T(8,128)(2,1)S(1)}, u32[]{:S(2)}) copy-start(bf16[3,2,2,192,96]{4,3,2,1,0:T(8,128)(2,1)S(1)} %collective-permute-done.1) | copy-start | bytes 1327108
  23.4 11.1 collective-permute-start.2
  34.5 22.3 %copy-start.3 = (bf16[3,2,2,192,96]{4,3,2,1,0:T(8,128)(2,1)}, bf16[3,2,2,192,96]{4,3,2,1,0:T(8,128)(2,1)S(1)}, u32[]{:S(2)}) copy-start(bf16[3,2,2,192,96]{4,3,2,1,0:T(8,128)(2,1)S(1)} %collective-permute-done.2) | copy-start | bytes 1327108
  34.5 11.1 collective-permute-start.3
  45.6 13.1 %copy-start.5 = (bf16[3,2,2,192,96]{4,3,2,1,0:T(8,128)(2,1)}, bf16[3,2,2,192,96]{4,3,2,1,0:T(8,128)(2,1)S(1)}, u32[]{:S(2)}) copy-start(bf16[3,2,2,192,96]{4,3,2,1,0:T(8,128)(2,1)S(1)} %collective-permute-done.3) | copy-start | bytes 1327108
  45.6 11.2 collective-permute-start.4
  56.8 33.4 %collective-permute-start.5 = (bf16[3,2,2,192,96]{4,3,2,1,0:T(8,128)(2,1)}, bf16[3,2,2,192,96]{4,3,2,1,0:T(8,128)(2,1)}, u32[]{:S(2)}, u32[]{:S(2)}) collective-permute-start(bf16[3,2,2,192,96]{4,3,2,1,0:T(8,128)(2,1)} %collective-permute-done.4), channel_id=1, source_target_pairs={{0,4},{4,8},{8,12},{12,16},{16,20},{20,24},{24,28},{28,0},{1,5},{5... | collective-permute-start | bytes 1327112 | tf_op jit(solution)/shard_map/ppermute | solution.py:16
  66.4 23.2 %copy-start.11 = (s32[2]{0:T(128)S(1)}, s32[2]{0:T(128)}, u32[]{:S(2)}) copy-start(s32[2]{0:T(128)} %param.11) | copy-start | bytes 28
  66.4 120.5 %copy-start.8 = (s32[768]{0:T(1024)S(1)}, s32[768]{0:T(1024)}, u32[]{:S(2)}) copy-start(s32[768]{0:T(1024)} %param.10) | copy-start | bytes 9220
  90.3 760.9 %collective-permute-start.6 = (bf16[3,2,2,192,96]{4,3,2,1,0:T(8,128)(2,1)}, bf16[3,2,2,192,96]{4,3,2,1,0:T(8,128)(2,1)}, u32[]{:S(2)}, u32[]{:S(2)}) collective-permute-start(bf16[3,2,2,192,96]{4,3,2,1,0:T(8,128)(2,1)} %collective-permute-done.5), channel_id=1, source_target_pairs={{0,4},{4,8},{8,12},{12,16},{16,20},{20,24},{24,28},{28,0},{1,5},{5... | collective-permute-start | bytes 1327112 | tf_op jit(solution)/shard_map/ppermute | solution.py:16
  189.7 126.8 %copy-start.2 = (bf16[3,2,2,192,96]{4,3,2,1,0:T(8,128)(2,1)S(1)}, bf16[3,2,2,192,96]{4,3,2,1,0:T(8,128)(2,1)}, u32[]{:S(2)}) copy-start(bf16[3,2,2,192,96]{4,3,2,1,0:T(8,128)(2,1)} %copy-done.1) | copy-start | bytes 1327108
  316.5 127.2 %copy-start.4 = (bf16[3,2,2,192,96]{4,3,2,1,0:T(8,128)(2,1)S(1)}, bf16[3,2,2,192,96]{4,3,2,1,0:T(8,128)(2,1)}, u32[]{:S(2)}) copy-start(bf16[3,2,2,192,96]{4,3,2,1,0:T(8,128)(2,1)} %copy-done.3) | copy-start | bytes 1327108
  443.7 127.2 %copy-start.6 = (bf16[3,2,2,192,96]{4,3,2,1,0:T(8,128)(2,1)S(1)}, bf16[3,2,2,192,96]{4,3,2,1,0:T(8,128)(2,1)}, u32[]{:S(2)}) copy-start(bf16[3,2,2,192,96]{4,3,2,1,0:T(8,128)(2,1)} %copy-done.5) | copy-start | bytes 1327108
  851.2 128.3 %copy-start.7 = (bf16[2,192,768,1,1]{2,0,4,3,1:T(2,128)(2,1)S(1)}, bf16[2,192,768,1,1]{2,0,4,3,1:T(2,128)(2,1)}, u32[]{:S(2)}) copy-start(bf16[2,192,768,1,1]{2,0,4,3,1:T(2,128)(2,1)} %copy.93) | copy-start | bytes 1769476
  979.5 27.9 %copy-start.9 = (f32[2]{0:T(128)S(1)}, f32[2]{0:T(128)}, u32[]{:S(2)}) copy-start(f32[2]{0:T(128)} %param.13) | copy-start | bytes 28
  979.5 27.9 %copy-start.10 = (f32[2]{0:T(128)S(1)}, f32[2]{0:T(128)}, u32[]{:S(2)}) copy-start(f32[2]{0:T(128)} %param.12) | copy-start | bytes 28
  1003.7 8.4 all-to-all-start
  1012.2 182.1 %all-to-all-start.2 = ((bf16[2,192,768]{1,0,2:T(2,128)(2,1)}), bf16[2,192,768]{1,0,2:T(2,128)(2,1)S(1)}, u32[]{:S(2)}, u32[]{:S(2)}) async-start(bf16[2,192,768]{1,0,2:T(2,128)(2,1)} %broadcast_select_fusion), calls=%async_computation.2 | async-start | bytes 1572864 | tf_op jit(solution)/shard_map/all_to_all | solution.py:127
  1194.3 7.9 all-to-all-start.1
